TPU v7x, 32 devices: a whole 2x2x4 slice. The times are simulated.
32 devices in a mesh: tm: 4 (over x, core), batch: 8 (over z, y).
Axes of the slice: x: 2, y: 2, z: 4, core: 2. Of those that a mesh axis runs over, the one named last changes fastest.
Arguments:
- initial_state: float32 [2048, 256], P('batch'), may hold values from -6 to 6
- increments: float32 [32, 2048, 256], P('tm', 'batch'), may hold values from -1.5 to 1.5
- cotangents: float32 [32, 2048, 256], P('tm', 'batch'), may hold values from -1.5 to 1.5
- drift_inner: bfloat16 [256, 1024], replicated, may hold values from -0.375 to 0.375
- drift_hidden: float32 [1024], replicated, may hold values from -3 to 3
- drift_outer: bfloat16 [1024, 256], replicated, may hold values from -0.1875 to 0.1875
- drift_offset: float32 [256], replicated, may hold values from -3 to 3
- noise_inner: bfloat16 [256, 1024], replicated, may hold values from -0.375 to 0.375
- noise_hidden: float32 [1024], replicated, may hold values from -3 to 3
- noise_outer: bfloat16 [1024, 256], replicated, may hold values from -0.1875 to 0.1875
- noise_offset: float32 [256], replicated, may hold values from -4 to 4
Outputs:
- states: float32 [32, 2048, 256], P('tm', 'batch')
- adjoints: float32 [32, 2048, 256], P('tm', 'batch')
- drift_inner_grad: float32 [256, 1024], replicated
- drift_hidden_grad: float32 [1024], replicated
- drift_outer_grad: float32 [1024, 256], replicated
- drift_offset_grad: float32 [256], replicated
- noise_inner_grad: float32 [256, 1024], replicated
- noise_hidden_grad: float32 [1024], replicated
- noise_outer_grad: float32 [1024, 256], replicated
- noise_offset_grad: float32 [256], replicated
All inputs are finite; a program needn't handle non-finite values.
Results may differ from a plain program's by a relative error of at most 0.0095.
Values sent between devices are 32-bit elements; how exact they have to be, the bound alone decides.
No kernel may reach another device: no remote copies, remote signals or barrier semaphores. Data moves between devices by JAX's collectives and lax.ppermute only.
A program may use at most 128 MiB of HBM per device.

v0:
```python
import math
import jax
import jax.numpy as jnp
from jax import lax
from jax.sharding import PartitionSpec as P

L = 256
H = 1024
delta_time = 0.05


def shifted(block, axis, distance):
    devices = range(lax.axis_size(axis))
    route = [(i - distance, i) for i in devices if i - distance in devices]
    return lax.ppermute(block, axis, route)


def matmul(left, right):
    return jnp.dot(left, right, preferred_element_type=jnp.float32)


def matmul_transposed(left, right):
    return lax.dot_general(
        left, right, (((1,), (1,)), ((), ())), preferred_element_type=jnp.float32
    )


def matmul_rows(left, right):
    return lax.dot_general(
        left, right, (((0,), (0,)), ((), ())), preferred_element_type=jnp.float32
    )


def advance(state, noise, params):
    (
        drift_inner,
        drift_hidden,
        drift_outer,
        drift_offset,
        noise_inner,
        noise_hidden,
        noise_outer,
        noise_offset,
    ) = params
    state_low = state.astype(jnp.bfloat16)
    hidden_drift = jnp.tanh(matmul(state_low, drift_inner) + drift_hidden).astype(jnp.bfloat16)
    hidden_noise = jnp.tanh(matmul(state_low, noise_inner) + noise_hidden).astype(jnp.bfloat16)
    drift = matmul(hidden_drift, drift_outer) + drift_offset
    spread = jax.nn.sigmoid(matmul(hidden_noise, noise_outer) + noise_offset)
    return (
        state + delta_time * drift + spread * noise,
        (state_low, hidden_drift, hidden_noise, spread),
    )


def retreat(adjoint_next, state, noise, params):
    (
        drift_inner,
        drift_hidden,
        drift_outer,
        drift_offset,
        noise_inner,
        noise_hidden,
        noise_outer,
        noise_offset,
    ) = params
    unused, saved = advance(state, noise, params)
    state_low, hidden_drift, hidden_noise, spread = saved
    drift_grad = delta_time * adjoint_next
    noise_grad = adjoint_next * noise * spread * (1.0 - spread)
    drift_low = drift_grad.astype(jnp.bfloat16)
    noise_low = noise_grad.astype(jnp.bfloat16)
    back_drift = matmul_transposed(drift_low, drift_outer) * (
        1.0 - jnp.square(hidden_drift.astype(jnp.float32))
    )
    back_noise = matmul_transposed(noise_low, noise_outer) * (
        1.0 - jnp.square(hidden_noise.astype(jnp.float32))
    )
    back_drift_low = back_drift.astype(jnp.bfloat16)
    back_noise_low = back_noise.astype(jnp.bfloat16)
    adjoint = (
        adjoint_next
        + matmul_transposed(back_drift_low, drift_inner)
        + matmul_transposed(back_noise_low, noise_inner)
    )
    grads = (
        matmul_rows(state_low, back_drift_low),
        jnp.sum(back_drift, 0),
        matmul_rows(hidden_drift, drift_low),
        jnp.sum(drift_grad, 0),
        matmul_rows(state_low, back_noise_low),
        jnp.sum(back_noise, 0),
        matmul_rows(hidden_noise, noise_low),
        jnp.sum(noise_grad, 0),
    )
    return (adjoint, grads)


def squares(grads):
    total = jnp.sum(jnp.square(grads[0]))
    for entry in grads[1:]:
        total = total + jnp.sum(jnp.square(entry))
    return total


def clip_factor(total):
    limit = 0.5 * math.sqrt(4 * L * H + 2 * H + 2 * L)
    return jnp.minimum(1.0, limit / jnp.sqrt(total))


def shards(
    initial_state,
    increments,
    cotangents,
    drift_inner,
    drift_hidden,
    drift_outer,
    drift_offset,
    noise_inner,
    noise_hidden,
    noise_outer,
    noise_offset,
):
    params = (
        drift_inner,
        drift_hidden,
        drift_outer,
        drift_offset,
        noise_inner,
        noise_hidden,
        noise_outer,
        noise_offset,
    )
    segments = lax.axis_size("tm")
    segment = lax.axis_index("tm")
    steps_here, rows, width = increments.shape
    blocks = 2
    block_rows = rows // blocks
    rounds = blocks + segments - 1

    def run_forward(operand):
        start_state, block, states, entries = operand
        offset = block * block_rows
        noise_block = lax.dynamic_slice_in_dim(increments, offset, block_rows, 1)
        state = start_state
        produced = []
        for index in range(steps_here):
            state, unused = advance(state, noise_block[index], params)
            produced.append(state)
        states = lax.dynamic_update_slice_in_dim(states, jnp.stack(produced), offset, 1)
        entries = lax.dynamic_update_slice_in_dim(entries, start_state, offset, 0)
        return (state, states, entries)

    def skip_forward(operand):
        start_state, block, states, entries = operand
        return (jnp.zeros_like(start_state), states, entries)

    def forward_round(turn, carry):
        incoming, states, entries = carry
        block = turn - segment
        valid = (block >= 0) & (block < blocks)
        clamped = jnp.clip(block, 0, blocks - 1)
        own = lax.dynamic_slice_in_dim(initial_state, clamped * block_rows, block_rows, 0)
        start_state = jnp.where(segment == 0, own, incoming)
        outgoing, states, entries = lax.cond(
            valid, run_forward, skip_forward, (start_state, clamped, states, entries)
        )
        incoming = shifted(outgoing, "tm", 1)
        return (incoming, states, entries)

    start = (
        jnp.zeros((block_rows, width), jnp.float32),
        jnp.zeros_like(increments),
        jnp.zeros_like(initial_state),
    )
    unused, states, entries = lax.fori_loop(0, rounds, forward_round, start)

    def run_backward(operand):
        adjoint, block, adjoints, totals = operand
        offset = block * block_rows
        noise_block = lax.dynamic_slice_in_dim(increments, offset, block_rows, 1)
        cotangent_block = lax.dynamic_slice_in_dim(cotangents, offset, block_rows, 1)
        state_block = lax.dynamic_slice_in_dim(states, offset, block_rows, 1)
        entry = lax.dynamic_slice_in_dim(entries, offset, block_rows, 0)
        column = [None] * steps_here
        for index in reversed(range(steps_here)):
            before = entry if index == 0 else state_block[index - 1]
            adjoint, grads = retreat(
                adjoint + cotangent_block[index], before, noise_block[index], params
            )
            totals = tuple((a + b for a, b in zip(totals, grads)))
            column[index] = adjoint
        adjoints = lax.dynamic_update_slice_in_dim(adjoints, jnp.stack(column), offset, 1)
        return (adjoint, adjoints, totals)

    def skip_backward(operand):
        adjoint, block, adjoints, totals = operand
        return (jnp.zeros_like(adjoint), adjoints, totals)

    def backward_round(turn, carry):
        incoming, adjoints, totals = carry
        block = turn - (segments - 1 - segment)
        valid = (block >= 0) & (block < blocks)
        clamped = jnp.clip(block, 0, blocks - 1)
        outgoing, adjoints, totals = lax.cond(
            valid, run_backward, skip_backward, (incoming, clamped, adjoints, totals)
        )
        incoming = shifted(outgoing, "tm", -1)
        return (incoming, adjoints, totals)

    blank = tuple((jnp.zeros(p.shape, jnp.float32) for p in params))
    start = (jnp.zeros((block_rows, width), jnp.float32), jnp.zeros_like(increments), blank)
    unused, adjoints, totals = lax.fori_loop(0, rounds, backward_round, start)
    summed = lax.psum(
        (totals[0], totals[1], totals[2], totals[3], totals[4], totals[5], totals[6], totals[7]),
        ("tm", "batch"),
    )
    factor = clip_factor(squares(summed))
    result = tuple((entry * factor for entry in summed))
    return (
        states,
        adjoints,
        result[0],
        result[1],
        result[2],
        result[3],
        result[4],
        result[5],
        result[6],
        result[7],
    )


def solution(mesh):
    placed = (
        P("batch", None),
        P("tm", "batch", None),
        P("tm", "batch", None),
        P(),
        P(),
        P(),
        P(),
        P(),
        P(),
        P(),
        P(),
    )
    return jax.shard_map(
        shards,
        mesh=mesh,
        in_specs=placed,
        out_specs=(
            P("tm", "batch", None),
            P("tm", "batch", None),
            P(),
            P(),
            P(),
            P(),
            P(),
            P(),
            P(),
            P(),
        ),
        check_vma=False,
    )
```

profile of v0, /device:TPU:0, one launch (start us, length us, event | category | flops | bytes accessed | tf_op | source)
XLA Modules:
  0.0 786.6 jit_solution(2424366928954173790)
XLA Ops:
  9.5 93.3 %while.51 = (s32[]{:T(128)}, f32[128,256]{1,0:T(8,128)S(1)}, f32[8,256,256]{2,1,0:T(8,128)}, bf16[256,256]{1,0:T(8,128)(2,1)}, s32[]{:T(128)}, /*index=5*/pred[]...) while((s32[]{:T(128)}, f32[128,256]{1,0:T(8,128)S(1)}, ...), condition=%wide.region_3.4_spmd, body=%wide.region_0.3_spmd.sunk | while | flops 2154594304 | bytes 28394616 | solution.py:176
  9.5 17.4 %conditional.4 = (f32[128,256]{1,0:T(8,128)}, f32[8,256,256]{2,1,0:T(8,128)}, bf16[256,256]{1,0:T(8,128)(2,1)}) conditional(s32[]{:T(128)} %convert_element_type.851, (f32[8,256,256]{2,1,0:T(8,128)}, bf16[256,256]{1,0:T(8,128)(2,1)}) %tuple.170, (pred[]{:T(512)}, s32[]{:T(128)}, f32[256,256]{1,0:T(8,128)}, f32[128,256]{1,0:T(8,128)S(1)}, ...), branch_computations={%region_1.1_spmd, %region_2.2_spmd} | conditional | flops 2154594304 | bytes 27869942 | solution.py:165
  29.4 17.4 %conditional.4 = (f32[128,256]{1,0:T(8,128)}, f32[8,256,256]{2,1,0:T(8,128)}, bf16[256,256]{1,0:T(8,128)(2,1)}) conditional(s32[]{:T(128)} %convert_element_type.851, (f32[8,256,256]{2,1,0:T(8,128)}, bf16[256,256]{1,0:T(8,128)(2,1)}) %tuple.170, (pred[]{:T(512)}, s32[]{:T(128)}, f32[256,256]{1,0:T(8,128)}, f32[128,256]{1,0:T(8,128)S(1)}, ...), branch_computations={%region_1.1_spmd, %region_2.2_spmd} | conditional | flops 2154594304 | bytes 27869942 | solution.py:165
  50.9 19.7 %collective-permute-start = (f32[128,256]{1,0:T(8,128)}, f32[128,256]{1,0:T(8,128)S(1)}, u32[]{:S(2)}, u32[]{:S(2)}) collective-permute-start(f32[128,256]{1,0:T(8,128)} %get-tuple-element.1600), channel_id=1, source_target_pairs={{0,8},{8,16},{16,24},{1,9},{9,17},{17,25},{2,10},{10,18},{18,26},{... | collective-permute-start | bytes 393224 | tf_op jit(solution)/shard_map/while/body/eval_jaxpr/ppermute | solution.py:15
  72.5 5.3 collective-permute-start
  79.6 22.0 %collective-permute-start = (f32[128,256]{1,0:T(8,128)}, f32[128,256]{1,0:T(8,128)S(1)}, u32[]{:S(2)}, u32[]{:S(2)}) collective-permute-start(f32[128,256]{1,0:T(8,128)} %get-tuple-element.1600), channel_id=1, source_target_pairs={{0,8},{8,16},{16,24},{1,9},{9,17},{17,25},{2,10},{10,18},{18,26},{... | collective-permute-start | bytes 393224 | tf_op jit(solution)/shard_map/while/body/eval_jaxpr/ppermute | solution.py:15
  102.8 2.7 convert.30
  112.6 504.2 %while.52 = (s32[]{:T(128)}, f32[128,256]{1,0:T(8,128)S(1)}, f32[8,256,256]{2,1,0:T(8,128)}, f32[256,1024]{1,0:T(8,128)S(1)}, f32[1024]{0:T(1024)}, /*index=5*/f...) while((s32[]{:T(128)}, f32[128,256]{1,0:T(8,128)S(1)}, ...), condition=%wide.region_39.40_spmd, body=%wide.region_4.39_spmd.sunk | while | flops 5935726592 | bytes 240598432 | solution.py:213
  114.6 5.1 collective-permute-done.1
  121.7 16.1 %collective-permute-done.1 = f32[128,256]{1,0:T(8,128)S(1)} collective-permute-done((f32[128,256]{1,0:T(8,128)}, f32[128,256]{1,0:T(8,128)S(1)}, u32[]{:S(2)}, u32[]{:S(2)}) %collective-permute-start.1) | collective-permute-done | bytes 131104 | tf_op jit(solution)/shard_map/while/body/eval_jaxpr/ppermute | solution.py:15
  139.7 280.0 %collective-permute-done.1 = f32[128,256]{1,0:T(8,128)S(1)} collective-permute-done((f32[128,256]{1,0:T(8,128)}, f32[128,256]{1,0:T(8,128)S(1)}, u32[]{:S(2)}, u32[]{:S(2)}) %collective-permute-start.1) | collective-permute-done | bytes 131104 | tf_op jit(solution)/shard_map/while/body/eval_jaxpr/ppermute | solution.py:15
  419.8 92.9 %conditional.5 = (f32[128,256]{1,0:T(8,128)S(1)}, f32[8,256,256]{2,1,0:T(8,128)}, f32[256,1024]{1,0:T(8,128)S(1)}, f32[1024]{0:T(1024)}, f32[1024,256]{1,0:T(8,1...) conditional(s32[]{:T(128)} %convert_element_type.852, ...), branch_computations={%region_5.5_spmd, %region_6.38_spmd} | conditional | flops 5935726592 | bytes 239549264 | solution.py:205
  428.0 2.5 multiply_reduce_fusion.6
  448.2 2.6 multiply_reduce_fusion.4
  459.3 2.6 multiply_reduce_fusion.3
  470.4 2.6 multiply_reduce_fusion.2
  514.6 5.2 collective-permute-done.1
  519.8 92.9 %conditional.5 = (f32[128,256]{1,0:T(8,128)S(1)}, f32[8,256,256]{2,1,0:T(8,128)}, f32[256,1024]{1,0:T(8,128)S(1)}, f32[1024]{0:T(1024)}, f32[1024,256]{1,0:T(8,1...) conditional(s32[]{:T(128)} %convert_element_type.852, ...), branch_computations={%region_5.5_spmd, %region_6.38_spmd} | conditional | flops 5935726592 | bytes 239549264 | solution.py:205
  548.3 2.6 multiply_reduce_fusion.4
  559.4 2.6 multiply_reduce_fusion.3
  570.5 2.6 multiply_reduce_fusion.2
  617.8 42.0 %all-reduce = (f32[1024]{0:T(1024)S(1)}, f32[256]{0:T(256)S(1)}, f32[1024]{0:T(1024)S(1)}, f32[256]{0:T(256)S(1)}) all-reduce(f32[1024]{0:T(1024)} %get-tuple-element.1132, f32[256]{0:T(256)} %get-tuple-element.1134, f32[1024]{0:T(1024)} %get-tuple-element.1136, ...), channel_id=1, replica_groups=mesh['tm'=4,'batch'=8] {'tm','batch'}, use_global_device_ids=true, to_apply=%region_42.43 | all-reduce | flops 2560 | bytes 20480 | tf_op jit(solution)/shard_map/psum | solution.py:214
  661.7 101.5 %all-reduce.4.cloned.1.call-done = (f32[256,1024]{1,0:T(8,128)}, f32[1024,256]{1,0:T(8,128)}, f32[256,1024]{1,0:T(8,128)}, f32[1024,256]{1,0:T(8,128)}) async-done(((f32[256,1024]{1,0:T(8,128)}, f32[1024,256]{1,0:T(8,128)}, f32[256,1024]{1,0:T(8,128)}, f32[1024,256]{1,0:T(8,128)}), (f32[256,1024]{1,0:T(8,128)}, f32[1024,256]{1,0:T(8,128)}, f32[256,1024]{1,0:T(8,128)}, ...) | async-done | bytes 4194320 | tf_op jit(solution)/shard_map/psum | solution.py:214
  763.2 2.6 multiply_reduce_fusion.8
  (629 shorter events, 246.1 us)
Async XLA Ops:
  7.2 756.0 %all-reduce.4.cloned.1.call-start = ((), (), s32[]{:S(2)}) async-start(), calls=%async_computation | async-start | bytes 8388608 | tf_op jit(solution)/shard_map/psum | solution.py:214
  27.0 2.5 collective-permute-start
  46.8 3.4 collective-permute-start
  50.9 20.9 %collective-permute-start = (f32[128,256]{1,0:T(8,128)}, f32[128,256]{1,0:T(8,128)S(1)}, u32[]{:S(2)}, u32[]{:S(2)}) collective-permute-start(f32[128,256]{1,0:T(8,128)} %get-tuple-element.1600), channel_id=1, source_target_pairs={{0,8},{8,16},{16,24},{1,9},{9,17},{17,25},{2,10},{10,18},{18,26},{... | collective-permute-start | bytes 393224 | tf_op jit(solution)/shard_map/while/body/eval_jaxpr/ppermute | solution.py:15
  72.5 6.5 collective-permute-start
  79.6 23.2 %collective-permute-start = (f32[128,256]{1,0:T(8,128)}, f32[128,256]{1,0:T(8,128)S(1)}, u32[]{:S(2)}, u32[]{:S(2)}) collective-permute-start(f32[128,256]{1,0:T(8,128)} %get-tuple-element.1600), channel_id=1, source_target_pairs={{0,8},{8,16},{16,24},{1,9},{9,17},{17,25},{2,10},{10,18},{18,26},{... | collective-permute-start | bytes 393224 | tf_op jit(solution)/shard_map/while/body/eval_jaxpr/ppermute | solution.py:15
  113.3 6.3 collective-permute-start.1
  120.4 17.4 %collective-permute-start.1 = (f32[128,256]{1,0:T(8,128)}, f32[128,256]{1,0:T(8,128)S(1)}, u32[]{:S(2)}, u32[]{:S(2)}) collective-permute-start(f32[128,256]{1,0:T(8,128)} %copy-done.65), channel_id=1, source_target_pairs={{8,0},{16,8},{24,16},{9,1},{17,9},{25,17},{10,2},{18,10},{26,18},{... | collective-permute-start | bytes 393224 | tf_op jit(solution)/shard_map/while/body/eval_jaxpr/ppermute | solution.py:15
  138.4 281.3 %collective-permute-start.1 = (f32[128,256]{1,0:T(8,128)}, f32[128,256]{1,0:T(8,128)S(1)}, u32[]{:S(2)}, u32[]{:S(2)}) collective-permute-start(f32[128,256]{1,0:T(8,128)} %copy-done.65), channel_id=1, source_target_pairs={{8,0},{16,8},{24,16},{9,1},{17,9},{25,17},{10,2},{18,10},{26,18},{... | collective-permute-start | bytes 393224 | tf_op jit(solution)/shard_map/while/body/eval_jaxpr/ppermute | solution.py:15
  430.5 6.4 copy-start.36
  440.5 6.0 copy-start.38
  448.2 4.6 copy-start.6
  450.9 6.8 copy-start.40
  459.3 4.7 copy-start.7
  462.0 6.8 copy-start.42
  473.1 6.8 copy-start.44
  513.3 6.5 collective-permute-start.1
  530.6 6.4 copy-start.36
  540.6 6.0 copy-start.38
  550.9 6.8 copy-start.40
  559.4 4.7 copy-start.7
  562.0 6.8 copy-start.42
  573.1 6.8 copy-start.44
  613.4 3.4 collective-permute-start.1
  (161 other events, 331.7 us)
Sparse Core Ops, SparseCore 0:
  618.0 145.2 all-reduce.3
where the time goes:
time: 789 us; the launch traced here: 787 us
  waiting for transfers between devices  416 us (53%)
  matrix products  175 us (22%)
  starting transfers between devices  57 us (7%)
  local copies, waits for them, and re-layouts  46.9 us (6%)
  blocking collectives  42 us (5%)
  other arithmetic  27.2 us (3%)
  between operations  19.4 us (2%)
    ppermute x10, waiting for transfers between devices, shifted(): return lax.ppermute(block, axis, route)  314 us
    psum x1, waiting for transfers between devices, shards(): lax.psum((totals[0], totals[1], totals[2], totals[3], totals[4], totals[5...  102 us
    dot_general x64, matrix products, matmul_transposed(): lax.dot_general(left, right, (((1,), (1,)), ((), ())), preferred_element_...  69.6 us
    dot_general x80, matrix products, matmul(): return jnp.dot(left, right, preferred_element_type=jnp.float32)  66.4 us
    ppermute x10, starting transfers between devices, shifted(): return lax.ppermute(block, axis, route)  57 us
    psum x1, blocking collectives, shards(): lax.psum((totals[0], totals[1], totals[2], totals[3], totals[4], totals[5...  42 us
    dot_general x64, matrix products, matmul_rows(): lax.dot_general(left, right, (((0,), (0,)), ((), ())), preferred_element_...  39.4 us
    cond x328, local copies, waits for them, and re-layouts  26.8 us
  transfers between devices with their start and end apart: 11, of which 11 were waited for; matrix products, arithmetic and copies ran while one was open for 0% of the time, Pallas kernels for 0%

commit v1 on v0

--- a/solution.py
+++ b/solution.py
@@ -1,3 +1,4 @@
+import functools
 import math
 import jax
 import jax.numpy as jnp
@@ -7,6 +8,14 @@
 L = 256
 H = 1024
 delta_time = 0.05
+
+
+def _step_on_roots(target, a_name, peer_axis):
+    r_now = lax.psum(target, a_name)
+    return lax.psum(r_now, peer_axis)
+
+
+fit_the_scenes = functools.partial(_step_on_roots, a_name="batch", peer_axis="tm")
 
 
 def shifted(block, axis, distance):
@@ -211,9 +220,8 @@
     blank = tuple((jnp.zeros(p.shape, jnp.float32) for p in params))
     start = (jnp.zeros((block_rows, width), jnp.float32), jnp.zeros_like(increments), blank)
     unused, adjoints, totals = lax.fori_loop(0, rounds, backward_round, start)
-    summed = lax.psum(
-        (totals[0], totals[1], totals[2], totals[3], totals[4], totals[5], totals[6], totals[7]),
-        ("tm", "batch"),
+    summed = fit_the_scenes(
+        (totals[0], totals[1], totals[2], totals[3], totals[4], totals[5], totals[6], totals[7])
     )
     factor = clip_factor(squares(summed))
     result = tuple((entry * factor for entry in summed))

time: 789 us -> 889 us (1.13)
  waiting for transfers between devices: 416 us -> 513 us
    psum x1 -> x2, waiting for transfers between devices: 102 us -> 198 us  [the longest x1 158 us: _step_on_roots(): r_now = lax.psum(target, a_name)]
    psum x1 -> x2, blocking collectives: 42 us -> 45.8 us  [the longest x1 34.9 us: _step_on_roots(): r_now = lax.psum(target, a_name)]
  transfers between devices with their start and end apart: 11 -> 12, of which waited for: 11 -> 12; matrix products, arithmetic and copies ran while one was open for 0% -> 0% of each run, Pallas kernels for 0% -> 0%
where the time goes in v1:
time: 889 us; the launch traced here: 887 us
  waiting for transfers between devices  513 us (58%)
  matrix products  175 us (20%)
  starting transfers between devices  57.1 us (6%)
  local copies, waits for them, and re-layouts  46.9 us (5%)
  blocking collectives  45.8 us (5%)
  other arithmetic  27.1 us (3%)
  between operations  19.4 us (2%)
    ppermute x10, waiting for transfers between devices, shifted(): return lax.ppermute(block, axis, route)  314 us
    psum x1, waiting for transfers between devices, _step_on_roots(): r_now = lax.psum(target, a_name)  158 us
    dot_general x64, matrix products, matmul_transposed(): lax.dot_general(left, right, (((1,), (1,)), ((), ())), preferred_element_...  69.6 us
    dot_general x80, matrix products, matmul(): return jnp.dot(left, right, preferred_element_type=jnp.float32)  66.4 us
    ppermute x10, starting transfers between devices, shifted(): return lax.ppermute(block, axis, route)  57 us
    psum x1, waiting for transfers between devices, _step_on_roots(): return lax.psum(r_now, peer_axis)  39.8 us
    dot_general x64, matrix products, matmul_rows(): lax.dot_general(left, right, (((0,), (0,)), ((), ())), preferred_element_...  39.4 us
    psum x1, blocking collectives, _step_on_roots(): r_now = lax.psum(target, a_name)  34.9 us
  transfers between devices with their start and end apart: 12, of which 12 were waited for; matrix products, arithmetic and copies ran while one was open for 0% of the time, Pallas kernels for 0%

profile of v1, /device:TPU:0, one launch (start us, length us, event | category | flops | bytes accessed | tf_op | source)
XLA Modules:
  0.0 887.0 jit_solution(11368989560200339694)
XLA Ops:
  9.5 93.3 %while.51 = (s32[]{:T(128)}, f32[128,256]{1,0:T(8,128)S(1)}, f32[8,256,256]{2,1,0:T(8,128)}, bf16[256,256]{1,0:T(8,128)(2,1)}, s32[]{:T(128)}, /*index=5*/pred[]...) while((s32[]{:T(128)}, f32[128,256]{1,0:T(8,128)S(1)}, ...), condition=%wide.region_3.4_spmd, body=%wide.region_0.3_spmd.sunk | while | flops 2154594304 | bytes 28394616 | solution.py:185
  9.5 17.4 %conditional.4 = (f32[128,256]{1,0:T(8,128)}, f32[8,256,256]{2,1,0:T(8,128)}, bf16[256,256]{1,0:T(8,128)(2,1)}) conditional(s32[]{:T(128)} %convert_element_type.851, (f32[8,256,256]{2,1,0:T(8,128)}, bf16[256,256]{1,0:T(8,128)(2,1)}) %tuple.170, (pred[]{:T(512)}, s32[]{:T(128)}, f32[256,256]{1,0:T(8,128)}, f32[128,256]{1,0:T(8,128)S(1)}, ...), branch_computations={%region_1.1_spmd, %region_2.2_spmd} | conditional | flops 2154594304 | bytes 27869942 | solution.py:174
  29.4 17.4 %conditional.4 = (f32[128,256]{1,0:T(8,128)}, f32[8,256,256]{2,1,0:T(8,128)}, bf16[256,256]{1,0:T(8,128)(2,1)}) conditional(s32[]{:T(128)} %convert_element_type.851, (f32[8,256,256]{2,1,0:T(8,128)}, bf16[256,256]{1,0:T(8,128)(2,1)}) %tuple.170, (pred[]{:T(512)}, s32[]{:T(128)}, f32[256,256]{1,0:T(8,128)}, f32[128,256]{1,0:T(8,128)S(1)}, ...), branch_computations={%region_1.1_spmd, %region_2.2_spmd} | conditional | flops 2154594304 | bytes 27869942 | solution.py:174
  50.9 19.7 %collective-permute-start = (f32[128,256]{1,0:T(8,128)}, f32[128,256]{1,0:T(8,128)S(1)}, u32[]{:S(2)}, u32[]{:S(2)}) collective-permute-start(f32[128,256]{1,0:T(8,128)} %get-tuple-element.1608), channel_id=1, source_target_pairs={{0,8},{8,16},{16,24},{1,9},{9,17},{17,25},{2,10},{10,18},{18,26},{... | collective-permute-start | bytes 393224 | tf_op jit(solution)/shard_map/while/body/eval_jaxpr/ppermute | solution.py:24
  72.5 5.3 collective-permute-start
  79.6 22.0 %collective-permute-start = (f32[128,256]{1,0:T(8,128)}, f32[128,256]{1,0:T(8,128)S(1)}, u32[]{:S(2)}, u32[]{:S(2)}) collective-permute-start(f32[128,256]{1,0:T(8,128)} %get-tuple-element.1608), channel_id=1, source_target_pairs={{0,8},{8,16},{16,24},{1,9},{9,17},{17,25},{2,10},{10,18},{18,26},{... | collective-permute-start | bytes 393224 | tf_op jit(solution)/shard_map/while/body/eval_jaxpr/ppermute | solution.py:24
  102.8 2.7 convert.30
  112.6 504.2 %while.52 = (s32[]{:T(128)}, f32[128,256]{1,0:T(8,128)S(1)}, f32[8,256,256]{2,1,0:T(8,128)}, f32[256,1024]{1,0:T(8,128)S(1)}, f32[1024]{0:T(1024)}, /*index=5*/f...) while((s32[]{:T(128)}, f32[128,256]{1,0:T(8,128)S(1)}, ...), condition=%wide.region_39.40_spmd, body=%wide.region_4.39_spmd.sunk | while | flops 5935726592 | bytes 240598432 | solution.py:222
  114.6 5.1 collective-permute-done.1
  121.7 16.1 %collective-permute-done.1 = f32[128,256]{1,0:T(8,128)S(1)} collective-permute-done((f32[128,256]{1,0:T(8,128)}, f32[128,256]{1,0:T(8,128)S(1)}, u32[]{:S(2)}, u32[]{:S(2)}) %collective-permute-start.1) | collective-permute-done | bytes 131104 | tf_op jit(solution)/shard_map/while/body/eval_jaxpr/ppermute | solution.py:24
  139.7 280.0 %collective-permute-done.1 = f32[128,256]{1,0:T(8,128)S(1)} collective-permute-done((f32[128,256]{1,0:T(8,128)}, f32[128,256]{1,0:T(8,128)S(1)}, u32[]{:S(2)}, u32[]{:S(2)}) %collective-permute-start.1) | collective-permute-done | bytes 131104 | tf_op jit(solution)/shard_map/while/body/eval_jaxpr/ppermute | solution.py:24
  419.8 92.9 %conditional.5 = (f32[128,256]{1,0:T(8,128)S(1)}, f32[8,256,256]{2,1,0:T(8,128)}, f32[256,1024]{1,0:T(8,128)S(1)}, f32[1024]{0:T(1024)}, f32[1024,256]{1,0:T(8,1...) conditional(s32[]{:T(128)} %convert_element_type.852, ...), branch_computations={%region_5.5_spmd, %region_6.38_spmd} | conditional | flops 5935726592 | bytes 239549264 | solution.py:214
  448.2 2.6 multiply_reduce_fusion.4
  459.3 2.6 multiply_reduce_fusion.3
  470.4 2.6 multiply_reduce_fusion.2
  514.6 5.2 collective-permute-done.1
  519.8 92.9 %conditional.5 = (f32[128,256]{1,0:T(8,128)S(1)}, f32[8,256,256]{2,1,0:T(8,128)}, f32[256,1024]{1,0:T(8,128)S(1)}, f32[1024]{0:T(1024)}, f32[1024,256]{1,0:T(8,1...) conditional(s32[]{:T(128)} %convert_element_type.852, ...), branch_computations={%region_5.5_spmd, %region_6.38_spmd} | conditional | flops 5935726592 | bytes 239549264 | solution.py:214
  548.3 2.6 multiply_reduce_fusion.4
  559.4 2.6 multiply_reduce_fusion.3
  570.5 2.6 multiply_reduce_fusion.2
  617.9 158.4 %all-reduce.7.cloned.1.call-done = (f32[256,1024]{1,0:T(8,128)}, f32[1024,256]{1,0:T(8,128)}, f32[256,1024]{1,0:T(8,128)}, f32[1024,256]{1,0:T(8,128)}) async-done(((f32[256,1024]{1,0:T(8,128)}, f32[1024,256]{1,0:T(8,128)}, f32[256,1024]{1,0:T(8,128)}, f32[1024,256]{1,0:T(8,128)}), (f32[256,1024]{1,0:T(8,128)}, f32[1024,256]{1,0:T(8,128)}, f32[256,1024]{1,0:T(8,128)}, ...) | async-done | bytes 4194320 | tf_op jit(solution)/shard_map/psum | solution.py:14
  776.3 34.9 %all-reduce = (f32[1024]{0:T(1024)S(1)}, f32[256]{0:T(256)S(1)}, f32[1024]{0:T(1024)S(1)}, f32[256]{0:T(256)S(1)}) all-reduce(f32[1024]{0:T(1024)} %get-tuple-element.1132, f32[256]{0:T(256)} %get-tuple-element.1134, f32[1024]{0:T(1024)} %get-tuple-element.1136, f32[256]{0:T(256)} %get-tuple-element.1138), channel_id=1, replica_groups=mesh['tm'=4,'batch'=8] {'batch'}, use_global_device_ids=true, to_apply=%region_43.44 | all-reduce | flops 2560 | bytes 20480 | tf_op jit(solution)/shard_map/psum | solution.py:14
  811.2 10.9 %all-reduce.2 = (f32[1024]{0:T(1024)S(1)}, f32[256]{0:T(256)S(1)}, f32[1024]{0:T(1024)S(1)}, f32[256]{0:T(256)S(1)}) all-reduce(f32[1024]{0:T(1024)S(1)} %get-tuple-element.1217, f32[256]{0:T(256)S(1)} %get-tuple-element.1218, f32[1024]{0:T(1024)S(1)} %get-tuple-element.1219, ...), channel_id=1, replica_groups=mesh['tm'=4,'batch'=8] {'tm'}, use_global_device_ids=true, to_apply=%region_44.45 | all-reduce | flops 2560 | bytes 20480 | tf_op jit(solution)/shard_map/psum | solution.py:15
  823.9 39.8 %all-reduce.9.cloned.1.call-done = (f32[256,1024]{1,0:T(8,128)}, f32[1024,256]{1,0:T(8,128)}, f32[256,1024]{1,0:T(8,128)}, f32[1024,256]{1,0:T(8,128)}) async-done(((f32[256,1024]{1,0:T(8,128)}, f32[1024,256]{1,0:T(8,128)}, f32[256,1024]{1,0:T(8,128)}, f32[1024,256]{1,0:T(8,128)}), (f32[256,1024]{1,0:T(8,128)}, f32[1024,256]{1,0:T(8,128)}, f32[256,1024]{1,0:T(8,128)}, ...) | async-done | bytes 4194320 | tf_op jit(solution)/shard_map/psum | solution.py:15
  (633 shorter events, 251.2 us)
Async XLA Ops:
  7.2 769.0 %all-reduce.7.cloned.1.call-start = ((), (), s32[]{:S(2)}) async-start(), calls=%async_computation | async-start | bytes 8388608 | tf_op jit(solution)/shard_map/psum | solution.py:14
  27.0 2.5 collective-permute-start
  46.8 3.4 collective-permute-start
  50.9 20.9 %collective-permute-start = (f32[128,256]{1,0:T(8,128)}, f32[128,256]{1,0:T(8,128)S(1)}, u32[]{:S(2)}, u32[]{:S(2)}) collective-permute-start(f32[128,256]{1,0:T(8,128)} %get-tuple-element.1608), channel_id=1, source_target_pairs={{0,8},{8,16},{16,24},{1,9},{9,17},{17,25},{2,10},{10,18},{18,26},{... | collective-permute-start | bytes 393224 | tf_op jit(solution)/shard_map/while/body/eval_jaxpr/ppermute | solution.py:24
  72.5 6.5 collective-permute-start
  79.6 23.2 %collective-permute-start = (f32[128,256]{1,0:T(8,128)}, f32[128,256]{1,0:T(8,128)S(1)}, u32[]{:S(2)}, u32[]{:S(2)}) collective-permute-start(f32[128,256]{1,0:T(8,128)} %get-tuple-element.1608), channel_id=1, source_target_pairs={{0,8},{8,16},{16,24},{1,9},{9,17},{17,25},{2,10},{10,18},{18,26},{... | collective-permute-start | bytes 393224 | tf_op jit(solution)/shard_map/while/body/eval_jaxpr/ppermute | solution.py:24
  113.3 6.3 collective-permute-start.1
  120.4 17.4 %collective-permute-start.1 = (f32[128,256]{1,0:T(8,128)}, f32[128,256]{1,0:T(8,128)S(1)}, u32[]{:S(2)}, u32[]{:S(2)}) collective-permute-start(f32[128,256]{1,0:T(8,128)} %copy-done.65), channel_id=1, source_target_pairs={{8,0},{16,8},{24,16},{9,1},{17,9},{25,17},{10,2},{18,10},{26,18},{... | collective-permute-start | bytes 393224 | tf_op jit(solution)/shard_map/while/body/eval_jaxpr/ppermute | solution.py:24
  138.4 281.3 %collective-permute-start.1 = (f32[128,256]{1,0:T(8,128)}, f32[128,256]{1,0:T(8,128)S(1)}, u32[]{:S(2)}, u32[]{:S(2)}) collective-permute-start(f32[128,256]{1,0:T(8,128)} %copy-done.65), channel_id=1, source_target_pairs={{8,0},{16,8},{24,16},{9,1},{17,9},{25,17},{10,2},{18,10},{26,18},{... | collective-permute-start | bytes 393224 | tf_op jit(solution)/shard_map/while/body/eval_jaxpr/ppermute | solution.py:24
  430.5 6.4 copy-start.36
  440.5 6.0 copy-start.38
  450.9 6.8 copy-start.40
  459.3 4.7 copy-start.7
  462.0 6.8 copy-start.42
  473.1 6.8 copy-start.44
  513.3 6.5 collective-permute-start.1
  530.6 6.4 copy-start.36
  540.6 6.0 copy-start.38
  550.9 6.8 copy-start.40
  559.4 4.7 copy-start.7
  562.0 6.8 copy-start.42
  573.1 6.8 copy-start.44
  613.4 3.4 collective-permute-start.1
  617.8 245.8 %all-reduce.9.cloned.1.call-start = ((), (), s32[]{:S(2)}) async-start(), calls=%async_computation.1 | async-start | bytes 8388608 | tf_op jit(solution)/shard_map/psum | solution.py:15
  (162 other events, 336.3 us)
Sparse Core Ops, SparseCore 0:
  618.0 158.2 all-reduce.6
  778.8 84.7 all-reduce.8
